TPU v7x, 32 devices: a whole 2x2x4 slice. The times are simulated.
32 devices in a mesh: dp: 8 (over z, y), tensor: 4 (over x, core).
Axes of the slice: x: 2, y: 2, z: 4, core: 2. Of those that a mesh axis runs over, the one named last changes fastest.
Arguments:
- hidden: bfloat16 [128, 4096], P(('dp', 'tensor')), may hold values from -6 to 6
- shortcut: bfloat16 [128, 4096], P('dp'), may hold values from -6 to 6
- expert_ids: int32 [128, 2], P('dp'), may hold values from 0 to 7, all different within a row; in each aligned block of 16 rows (0 to 15, 16 to 31, ...) at most 6 rows name the same one
- route_weight: float32 [128, 2], P('dp'), may hold values from 0.1 to 1
- dense_gain: float32 [4096], replicated, may hold values from 0.5 to 1.5
- moe_gain: float32 [4096], replicated, may hold values from 0.5 to 1.5
- dense_gate: bfloat16 [4096, 8192], P(None, 'dp'), may hold values from -0.09375 to 0.09375
- dense_lift: bfloat16 [4096, 8192], P(None, 'dp'), may hold values from -0.09375 to 0.09375
- dense_down: bfloat16 [8192, 4096], P('dp'), may hold values from -0.0625 to 0.0625
- expert_gate: bfloat16 [4096, 65536], P(None, ('dp', 'tensor')), may hold values from -0.09375 to 0.09375
- expert_lift: bfloat16 [4096, 65536], P(None, ('dp', 'tensor')), may hold values from -0.09375 to 0.09375
- expert_down: bfloat16 [65536, 4096], P(('dp', 'tensor')), may hold values from -0.0625 to 0.0625
Outputs:
- mixed: bfloat16 [128, 4096], P(('dp', 'tensor'))
Inputs may be any that keep to these rules, and one draw needn't show every extreme that they name: `expert_ids`: the 2 experts of a token differ. In each aligned block of 16 rows (the tokens of one index of dp) no expert is named by more than 6 rows, and in every draw some expert is named by exactly 6 rows of some block; every expert is named somewhere.
All inputs are finite; a program needn't handle non-finite values.
Results may differ from a plain program's by a relative error of at most 0.006.
Values may be sent and summed in bfloat16 or wider, within the bound.
A program may use at most 128 MiB of HBM per device.

v0:
```python
import jax
import jax.numpy as jnp
from jax import lax
from jax.sharding import PartitionSpec as P

D = 4096
E = 8
TOP = 2
CAP = 6
EPSILON = 1e-05


def normalize(values_in, gain):
    values = values_in.astype(jnp.float32)
    scale = lax.rsqrt(jnp.mean(values * values, axis=-1, keepdims=True) + EPSILON)
    return (values * scale * gain).astype(jnp.bfloat16)


def local(
    hidden,
    shortcut,
    expert_ids,
    route_weight,
    dense_gain,
    moe_gain,
    dense_gate,
    dense_lift,
    dense_down,
    expert_gate,
    expert_lift,
    expert_down,
):
    normed = normalize(hidden, dense_gain)
    piece = lax.all_gather(normed, "dp", axis=0, tiled=True)
    gate_vals = jnp.dot(piece, dense_gate, preferred_element_type=jnp.float32)
    lift_vals = jnp.dot(piece, dense_lift, preferred_element_type=jnp.float32)
    dense_inner = (jax.nn.silu(gate_vals) * lift_vals).astype(jnp.bfloat16)
    dense_out = lax.psum_scatter(
        jnp.dot(dense_inner, dense_down, preferred_element_type=jnp.float32),
        "dp",
        scatter_dimension=0,
        tiled=True,
    )
    members = lax.axis_size("dp") // E
    token_count = shortcut.shape[0]
    moe_in = normalize(shortcut, moe_gain)
    flat = expert_ids.reshape(token_count * TOP)
    picked = (flat[:, None] == jnp.arange(E, dtype=jnp.int32)[None, :]).astype(jnp.int32)
    before = jnp.cumsum(picked, axis=0) - picked
    places = flat * CAP + jnp.sum(before * picked, axis=1)
    chosen = (places[:, None] == jnp.arange(E * CAP, dtype=jnp.int32)[None, :]).astype(jnp.float32)
    chosen = chosen.reshape(token_count, TOP, E * CAP)
    spread = jnp.sum(chosen, axis=1).astype(jnp.bfloat16)
    weighted = jnp.sum(chosen * route_weight[:, :, None], axis=1)
    buffer = lax.dot_general(
        spread, moe_in, (((0,), (0,)), ((), ())), preferred_element_type=jnp.float32
    )
    buffer = buffer.astype(jnp.bfloat16).reshape(E, CAP, D)
    outgoing = jnp.repeat(buffer, members, axis=0)
    arrived = lax.all_to_all(outgoing, "dp", split_axis=0, concat_axis=0, tiled=True)
    sources, count, width = arrived.shape
    rows_in = arrived.reshape(sources * count, width)
    gate_vals = jnp.dot(rows_in, expert_gate, preferred_element_type=jnp.float32)
    lift_vals = jnp.dot(rows_in, expert_lift, preferred_element_type=jnp.float32)
    inner = (jax.nn.silu(gate_vals) * lift_vals).astype(jnp.bfloat16)
    terms = jnp.dot(inner, expert_down, preferred_element_type=jnp.float32).astype(jnp.bfloat16)
    returned = lax.all_to_all(
        terms.reshape(sources, count, D), "dp", split_axis=0, concat_axis=0, tiled=True
    )
    summed = jnp.sum(returned.astype(jnp.float32).reshape(E, members, CAP, D), axis=1).reshape(
        E * CAP, D
    )
    moe_part = jnp.dot(
        weighted, summed, precision=lax.Precision.HIGHEST, preferred_element_type=jnp.float32
    )
    moe_out = lax.psum_scatter(moe_part, "tensor", scatter_dimension=0, tiled=True)
    return (hidden.astype(jnp.float32) + dense_out + moe_out).astype(jnp.bfloat16)


def solution(mesh):
    in_specs = (
        P(("dp", "tensor"), None),
        P("dp", None),
        P("dp", None),
        P("dp", None),
        P(),
        P(),
        P(None, "dp"),
        P(None, "dp"),
        P("dp", None),
        P(None, ("dp", "tensor")),
        P(None, ("dp", "tensor")),
        P(("dp", "tensor"), None),
    )
    out_specs = P(("dp", "tensor"), None)
    return jax.shard_map(local, mesh=mesh, in_specs=in_specs, out_specs=out_specs, check_vma=False)
```

profile of v0, /device:TPU:0, one launch (start us, length us, event | category | flops | bytes accessed | tf_op | source)
XLA Modules:
  0.0 215.8 jit_solution(18423160063778586891)
XLA Ops:
  6.5 0.8 copy.29
  7.3 0.1 eq.29
  7.4 0.1 fusion.27
  7.5 0.1 reduce_window_sum.11
  7.5 0.2 select_reduce_fusion.1
  7.7 0.1 reduce_sum.53
  7.8 0.1 copy.30
  7.9 0.7 multiply_add_fusion
  8.6 1.0 fusion.8
  9.6 0.8 convert_reduce_fusion
  10.4 1.2 convolution_convert_fusion.1
  11.6 0.9 reshape_broadcast_in_dim_reshape.3
  12.5 7.3 %all-to-all-start = ((bf16[8,6,4096]{2,1,0:T(8,128)(2,1)}), bf16[8,6,4096]{2,1,0:T(8,128)(2,1)S(1)}, u32[]{:S(2)}, u32[]{:S(2)}) async-start(bf16[8,6,4096]{2,1,0:T(8,128)(2,1)} %reshape_broadcast_in_dim_reshape.3), calls=%async_computation | async-start | bytes 1048576 | tf_op jit(solution)/shard_map/all_to_all | solution.py:60
  19.8 0.9 fusion.20
  20.8 0.9 fusion.26
  21.6 36.0 %all-gather = bf16[8,4,4096]{2,1,0:T(4,128)(2,1)S(1)} all-gather(bf16[1,4,4096]{2,1,0:T(4,128)(2,1)S(1)} %fusion.26), channel_id=1, replica_groups=mesh['dp'=8,'tensor'=4] {'dp'}, dimensions={0}, use_global_device_ids=true | all-gather | bytes 294912 | tf_op jit(solution)/shard_map/all_gather | solution.py:34
  57.6 0.1 reshape.55
  57.7 4.9 %fusion.31 = f32[32,1024]{1,0:T(8,128)S(1)} fusion(bf16[32,4096]{1,0:T(8,128)(2,1)S(1)} %reshape.55, bf16[4096,1024]{1,0:T(8,128)(2,1)} %param.18), kind=kOutput, calls=%fused_computation.47 | convolution fusion | flops 268435456 | bytes 8781824 | tf_op jit(solution)/shard_map/dot_general | solution.py:35
  62.6 0.0 all-to-all-done
  62.6 0.1 reshape.51
  62.8 8.8 %fusion.32 = f32[48,2048]{1,0:T(8,128)S(1)} fusion(bf16[48,4096]{1,0:T(8,128)(2,1)S(1)} %reshape.51, bf16[4096,2048]{1,0:T(8,128)(2,1)} %param.21), kind=kOutput, calls=%fused_computation.48 | convolution fusion | flops 805306368 | bytes 17563648 | tf_op jit(solution)/shard_map/dot_general | solution.py:63
  71.5 13.7 %convolution_convert_fusion = bf16[48,4096]{1,0:T(8,128)(2,1)S(1)} fusion(bf16[2048,4096]{1,0:T(8,128)(2,1)} %param.23, bf16[48,4096]{1,0:T(8,128)(2,1)S(1)} %reshape.51, bf16[4096,2048]{1,0:T(8,128)(2,1)} %param.22, f32[48,2048]{1,0:T(8,128)S(1)} %fusion.32), kind=kOutput, calls=%fused_computation | convolution fusion | flops 1611399168 | bytes 34734080 | tf_op jit(solution)/shard_map/dot_general | solution.py:66
  85.2 0.0 copy-start.2
  85.2 0.0 copy-start.1
  85.2 0.0 copy-start
  85.3 1.0 reshape.52
  86.2 3.5 %all-to-all-start.1 = ((bf16[8,6,4096]{2,1,0:T(8,128)(2,1)}), bf16[8,6,4096]{2,1,0:T(8,128)(2,1)S(1)}, u32[]{:S(2)}, u32[]{:S(2)}) async-start(bf16[8,6,4096]{2,1,0:T(8,128)(2,1)} %reshape.52), calls=%async_computation.1 | async-start | bytes 1048576 | tf_op jit(solution)/shard_map/all_to_all | solution.py:67
  89.7 0.0 all-reduce.5.cloned.1.call-start
  89.8 9.6 %fusion.2 = f32[32,4096]{1,0:T(8,128)} fusion(bf16[1024,4096]{1,0:T(8,128)(2,1)} %param.20, bf16[32,4096]{1,0:T(8,128)(2,1)S(1)} %reshape.55, bf16[4096,1024]{1,0:T(8,128)(2,1)} %param.19, f32[32,1024]{1,0:T(8,128)S(1)} %fusion.31), kind=kOutput, calls=%fused_computation.6 | convolution fusion | flops 537067520 | bytes 17694720 | tf_op jit(solution)/shard_map/dot_general | solution.py:39
  99.4 0.0 all-reduce.5.cloned.1.call-update
  99.4 0.0 all-reduce.7.cloned.1.call-start
  99.4 0.5 all-to-all-done.1
  99.9 0.1 reshape.53
  100.1 1.0 fusion.33
  101.1 0.0 all-reduce.7.cloned.1.call-update
  101.1 0.0 copy-done.2
  101.1 0.6 dynamic-slice
  101.7 0.0 copy-done.1
  101.7 0.6 dynamic-slice.2
  103.6 70.0 %all-reduce.5.cloned.1.call-done = f32[32,4096]{1,0:T(8,128)} async-done(((f32[32,4096]{1,0:T(8,128)}), f32[32,4096]{1,0:T(8,128)}) %all-reduce.5.cloned.1.call-update) | async-done | bytes 524304
  173.6 33.8 %all-reduce.7.cloned.1.call-done = f32[16,4096]{1,0:T(8,128)} async-done(((f32[16,4096]{1,0:T(8,128)}), f32[16,4096]{1,0:T(8,128)}) %all-reduce.7.cloned.1.call-update) | async-done | bytes 262160
  207.4 0.0 copy-done
  207.4 1.6 fusion.24
  (2 shorter events, 0.0 us)
Async XLA Ops:
  12.5 50.1 %all-to-all-start = ((bf16[8,6,4096]{2,1,0:T(8,128)(2,1)}), bf16[8,6,4096]{2,1,0:T(8,128)(2,1)S(1)}, u32[]{:S(2)}, u32[]{:S(2)}) async-start(bf16[8,6,4096]{2,1,0:T(8,128)(2,1)} %reshape_broadcast_in_dim_reshape.3), calls=%async_computation | async-start | bytes 1048576 | tf_op jit(solution)/shard_map/all_to_all | solution.py:60
  85.2 15.9 %copy-start.2 = (u32[32]{0:T(128)S(1)}, u32[32]{0:T(128)}, u32[]{:S(2)}) copy-start(u32[32]{0:T(128)} %constant.27) | copy-start | bytes 388
  85.2 16.5 %copy-start.1 = (u32[32]{0:T(128)S(1)}, u32[32]{0:T(128)}, u32[]{:S(2)}) copy-start(u32[32]{0:T(128)} %constant.31) | copy-start | bytes 388
  85.2 122.1 %copy-start = (bf16[4,4096]{1,0:T(4,128)(2,1)S(1)}, bf16[4,4096]{1,0:T(4,128)(2,1)}, u32[]{:S(2)}) copy-start(bf16[4,4096]{1,0:T(4,128)(2,1)} %param.12) | copy-start | bytes 98308
  86.2 13.7 %all-to-all-start.1 = ((bf16[8,6,4096]{2,1,0:T(8,128)(2,1)}), bf16[8,6,4096]{2,1,0:T(8,128)(2,1)S(1)}, u32[]{:S(2)}, u32[]{:S(2)}) async-start(bf16[8,6,4096]{2,1,0:T(8,128)(2,1)} %reshape.52), calls=%async_computation.1 | async-start | bytes 1048576 | tf_op jit(solution)/shard_map/all_to_all | solution.py:67
  89.7 83.8 %all-reduce.5.cloned.1.call-start = ((), (), s32[]{:S(2)}) async-start(), calls=%async_computation.2 | async-start | bytes 1048576
  99.4 108.0 %all-reduce.7.cloned.1.call-start = ((), (), s32[]{:S(2)}) async-start(), calls=%async_computation.3 | async-start | bytes 524288
Sparse Core Ops, SparseCore 0:
  99.5 73.9 all-reduce.4
  175.9 31.4 all-reduce.6
where the time goes:
time: 216 us
  waiting for transfers between devices  104 us (48%)
  matrix products  39.2 us (18%)
  blocking collectives  36 us (17%)
  between operations  14.8 us (7%)
  starting transfers between devices  10.9 us (5%)
  other arithmetic  6.21 us (3%)
  local copies, waits for them, and re-layouts  4.44 us (2%)
    unnamed x4, waiting for transfers between devices  104 us
    all_gather x1, blocking collectives, local(): piece = lax.all_gather(normed, 'dp', axis=0, tiled=True)  36 us
    dot_general x1, matrix products, local(): jnp.dot(inner, expert_down, preferred_element_type=jnp.float32)  13.7 us
    dot_general x1, matrix products, local(): jnp.dot(dense_inner, dense_down, preferred_element_type=jnp.float32)  9.6 us
    dot_general x1, matrix products, local(): jnp.dot(rows_in, expert_gate, preferred_element_type=jnp.float32)  8.79 us
    all_to_all x1, starting transfers between devices, local(): lax.all_to_all(outgoing, 'dp', split_axis=0, concat_axis=0, tiled=True)  7.31 us
    dot_general x1, matrix products, local(): gate_vals = jnp.dot(piece, dense_gate, preferred_element_type=jnp.float32)  4.92 us
  transfers between devices with their start and end apart: 4, of which 3 were waited for; matrix products, arithmetic and copies ran while one was open for 9% of the time, Pallas kernels for 0%

commit v1 on v0

--- a/solution.py
+++ b/solution.py
@@ -31,7 +31,17 @@
     expert_down,
 ):
     normed = normalize(hidden, dense_gain)
-    piece = lax.all_gather(normed, "dp", axis=0, tiled=True)
+    ndev = lax.psum(1, axis_name="dp")
+    low = [(b - 1, b) for b in range(1, ndev)] + [(ndev - 1, 0)]
+    parts_out = normed
+    entries = [parts_out]
+    ii = 0
+    while ii < ndev - 1:
+        parts_out = lax.ppermute(parts_out, axis_name="dp", perm=low)
+        entries += [parts_out]
+        ii += 1
+    small = jnp.concatenate([*reversed(entries)], axis=0)
+    piece = jnp.roll(small, (lax.axis_index("dp") + 1) * parts_out.shape[0], axis=0)
     gate_vals = jnp.dot(piece, dense_gate, preferred_element_type=jnp.float32)
     lift_vals = jnp.dot(piece, dense_lift, preferred_element_type=jnp.float32)
     dense_inner = (jax.nn.silu(gate_vals) * lift_vals).astype(jnp.bfloat16)

time: 216 us -> 222 us (1.028)
  waiting for transfers between devices: 104 us -> 142 us
  blocking collectives: 36 us -> 0 us
  starting transfers between devices: 10.9 us -> 14.7 us
    ppermute x0 -> x7, waiting for transfers between devices: none -> 37.5 us  [local(): parts_out = lax.ppermute(parts_out, axis_name='dp', perm=low)]
    all_gather x1 -> x0, blocking collectives: 36 us -> none  [local(): piece = lax.all_gather(normed, 'dp', axis=0, tiled=True)]
    ppermute x0 -> x7, starting transfers between devices: none -> 5.08 us  [local(): parts_out = lax.ppermute(parts_out, axis_name='dp', perm=low)]
  transfers between devices with their start and end apart: 4 -> 11, of which waited for: 3 -> 9; matrix products, arithmetic and copies ran while one was open for 9% -> 10% of each run, Pallas kernels for 0% -> 0%
where the time goes in v1:
time: 222 us; the launch traced here: 221 us
  waiting for transfers between devices  142 us (64%)
  matrix products  39.2 us (18%)
  between operations  14.8 us (7%)
  starting transfers between devices  14.7 us (7%)
  other arithmetic  6.2 us (3%)
  local copies, waits for them, and re-layouts  4.76 us (2%)
    unnamed x4, waiting for transfers between devices  104 us
    ppermute x7, waiting for transfers between devices, local(): parts_out = lax.ppermute(parts_out, axis_name='dp', perm=low)  37.5 us
    dot_general x1, matrix products, local(): jnp.dot(inner, expert_down, preferred_element_type=jnp.float32)  13.7 us
    dot_general x1, matrix products, local(): jnp.dot(dense_inner, dense_down, preferred_element_type=jnp.float32)  9.6 us
    dot_general x1, matrix products, local(): jnp.dot(rows_in, expert_gate, preferred_element_type=jnp.float32)  8.79 us
    all_to_all x1, starting transfers between devices, local(): lax.all_to_all(outgoing, 'dp', split_axis=0, concat_axis=0, tiled=True)  6 us
    ppermute x7, starting transfers between devices, local(): parts_out = lax.ppermute(parts_out, axis_name='dp', perm=low)  5.08 us
    dot_general x1, matrix products, local(): lift_vals = jnp.dot(piece, dense_lift, preferred_element_type=jnp.float32)  4.92 us
  transfers between devices with their start and end apart: 11, of which 9 were waited for; matrix products, arithmetic and copies ran while one was open for 10% of the time, Pallas kernels for 0%

profile of v1, /device:TPU:0, one launch (start us, length us, event | category | flops | bytes accessed | tf_op | source)
XLA Modules:
  0.0 221.4 jit_solution(14129256722780771900)
XLA Ops:
  6.5 0.9 fusion.17
  7.4 0.9 fusion.19
  8.3 3.0 %collective-permute-start = (bf16[4,4096]{1,0:T(4,128)(2,1)S(1)}, bf16[4,4096]{1,0:T(4,128)(2,1)S(1)}, u32[]{:S(2)}, u32[]{:S(2)}) collective-permute-start(bf16[4,4096]{1,0:T(4,128)(2,1)S(1)} %fusion.19), channel_id=1, source_target_pairs={{0,4},{4,8},{8,12},{12,16},{16,20},{20,24},{24,28},{28,0},{1,5},{5... | collective-permute-start | bytes 98312 | tf_op jit(solution)/shard_map/ppermute | solution.py:40
  11.4 0.8 copy.29
  12.1 0.1 eq.32
  12.2 0.1 fusion.28
  12.3 0.1 reduce_window_sum.11
  12.3 0.2 select_reduce_fusion.1
  12.5 0.1 reduce_sum.53
  12.6 0.1 copy.30
  12.7 0.7 multiply_add_fusion
  13.4 1.0 fusion.6
  14.4 1.8 collective-permute-done
  16.3 0.0 collective-permute-start.1
  16.3 0.8 convert_reduce_fusion
  17.0 5.8 %collective-permute-done.1 = bf16[4,4096]{1,0:T(4,128)(2,1)S(1)} collective-permute-done((bf16[4,4096]{1,0:T(4,128)(2,1)S(1)}, bf16[4,4096]{1,0:T(4,128)(2,1)S(1)}, u32[]{:S(2)}, u32[]{:S(2)}) %collective-permute-start.1) | collective-permute-done | bytes 32800 | tf_op jit(solution)/shard_map/ppermute | solution.py:40
  22.9 1.2 convolution_convert_fusion.1
  24.1 0.9 reshape_broadcast_in_dim_reshape.3
  25.0 6.0 %all-to-all-start = ((bf16[8,6,4096]{2,1,0:T(8,128)(2,1)}), bf16[8,6,4096]{2,1,0:T(8,128)(2,1)S(1)}, u32[]{:S(2)}, u32[]{:S(2)}) async-start(bf16[8,6,4096]{2,1,0:T(8,128)(2,1)} %reshape_broadcast_in_dim_reshape.3), calls=%async_computation | async-start | bytes 1048576 | tf_op jit(solution)/shard_map/all_to_all | solution.py:70
  31.0 2.0 collective-permute-start.3
  33.1 10.0 %collective-permute-done.3 = bf16[4,4096]{1,0:T(4,128)(2,1)S(1)} collective-permute-done((bf16[4,4096]{1,0:T(4,128)(2,1)S(1)}, bf16[4,4096]{1,0:T(4,128)(2,1)S(1)}, u32[]{:S(2)}, u32[]{:S(2)}) %collective-permute-start.3) | collective-permute-done | bytes 32800 | tf_op jit(solution)/shard_map/ppermute | solution.py:40
  43.1 6.6 %collective-permute-done.4 = bf16[4,4096]{1,0:T(4,128)(2,1)S(1)} collective-permute-done((bf16[4,4096]{1,0:T(4,128)(2,1)S(1)}, bf16[4,4096]{1,0:T(4,128)(2,1)S(1)}, u32[]{:S(2)}, u32[]{:S(2)}) %collective-permute-start.4) | collective-permute-done | bytes 32800 | tf_op jit(solution)/shard_map/ppermute | solution.py:40
  49.7 6.6 %collective-permute-done.5 = bf16[4,4096]{1,0:T(4,128)(2,1)S(1)} collective-permute-done((bf16[4,4096]{1,0:T(4,128)(2,1)S(1)}, bf16[4,4096]{1,0:T(4,128)(2,1)S(1)}, u32[]{:S(2)}, u32[]{:S(2)}) %collective-permute-start.5) | collective-permute-done | bytes 32800 | tf_op jit(solution)/shard_map/ppermute | solution.py:40
  56.3 6.6 %collective-permute-done.6 = bf16[4,4096]{1,0:T(4,128)(2,1)S(1)} collective-permute-done((bf16[4,4096]{1,0:T(4,128)(2,1)S(1)}, bf16[4,4096]{1,0:T(4,128)(2,1)S(1)}, u32[]{:S(2)}, u32[]{:S(2)}) %collective-permute-start.6) | collective-permute-done | bytes 32800 | tf_op jit(solution)/shard_map/ppermute | solution.py:40
  62.9 0.4 concatenate.6
  63.3 4.9 %fusion.9 = f32[32,1024]{1,0:T(8,128)S(1)} fusion(bf16[4096,1024]{1,0:T(8,128)(2,1)} %param.19, bf16[64,4096]{1,0:T(8,128)(2,1)S(1)} %concatenate.6, s32[]{:T(128)S(6)} %select_n.14), kind=kOutput, calls=%fused_computation.14 | convolution fusion | flops 268435456 | bytes 8781828 | tf_op jit(solution)/shard_map/dot_general | solution.py:46
  68.2 0.0 all-to-all-done
  68.2 0.1 reshape.51
  68.4 8.8 %fusion.35 = f32[48,2048]{1,0:T(8,128)S(1)} fusion(bf16[48,4096]{1,0:T(8,128)(2,1)S(1)} %reshape.51, bf16[4096,2048]{1,0:T(8,128)(2,1)} %param.21), kind=kOutput, calls=%fused_computation.46 | convolution fusion | flops 805306368 | bytes 17563648 | tf_op jit(solution)/shard_map/dot_general | solution.py:73
  77.2 13.7 %convolution_convert_fusion = bf16[48,4096]{1,0:T(8,128)(2,1)S(1)} fusion(bf16[2048,4096]{1,0:T(8,128)(2,1)} %param.23, bf16[48,4096]{1,0:T(8,128)(2,1)S(1)} %reshape.51, bf16[4096,2048]{1,0:T(8,128)(2,1)} %param.22, f32[48,2048]{1,0:T(8,128)S(1)} %fusion.35), kind=kOutput, calls=%fused_computation | convolution fusion | flops 1611399168 | bytes 34734080 | tf_op jit(solution)/shard_map/dot_general | solution.py:76
  90.8 0.0 copy-start.2
  90.9 0.0 copy-start.1
  90.9 0.0 copy-start
  90.9 1.0 reshape.52
  91.8 3.5 %all-to-all-start.1 = ((bf16[8,6,4096]{2,1,0:T(8,128)(2,1)}), bf16[8,6,4096]{2,1,0:T(8,128)(2,1)S(1)}, u32[]{:S(2)}, u32[]{:S(2)}) async-start(bf16[8,6,4096]{2,1,0:T(8,128)(2,1)} %reshape.52), calls=%async_computation.1 | async-start | bytes 1048576 | tf_op jit(solution)/shard_map/all_to_all | solution.py:77
  95.3 0.0 all-reduce.5.cloned.1.call-start
  95.4 9.6 %fusion.22 = f32[32,4096]{1,0:T(8,128)} fusion(bf16[1024,4096]{1,0:T(8,128)(2,1)} %param.20, f32[32,1024]{1,0:T(8,128)S(1)} %fusion.9, bf16[4096,1024]{1,0:T(8,128)(2,1)} %param.18, bf16[64,4096]{1,0:T(8,128)(2,1)S(1)} %concatenate.6, s32[]{:T(128)S(6)} %select_n.14), kind=kOutput, calls=%fused_computation.30 | convolution fusion | flops 537067520 | bytes 17694724 | tf_op jit(solution)/shard_map/dot_general | solution.py:49
  105.0 0.0 all-reduce.5.cloned.1.call-update
  105.0 0.0 all-reduce.7.cloned.1.call-start
  105.1 0.5 all-to-all-done.1
  105.5 0.1 reshape.53
  105.7 1.0 fusion.36
  106.7 0.0 all-reduce.7.cloned.1.call-update
  106.7 0.6 dynamic-slice.2
  107.3 0.6 dynamic-slice
  109.2 70.0 %all-reduce.5.cloned.1.call-done = f32[32,4096]{1,0:T(8,128)} async-done(((f32[32,4096]{1,0:T(8,128)}), f32[32,4096]{1,0:T(8,128)}) %all-reduce.5.cloned.1.call-update) | async-done | bytes 524304
  179.2 33.8 %all-reduce.7.cloned.1.call-done = f32[16,4096]{1,0:T(8,128)} async-done(((f32[16,4096]{1,0:T(8,128)}), f32[16,4096]{1,0:T(8,128)}) %all-reduce.7.cloned.1.call-update) | async-done | bytes 262160
  213.0 1.6 fusion.21
  (10 shorter events, 0.0 us)
Async XLA Ops:
  8.3 8.0 %collective-permute-start = (bf16[4,4096]{1,0:T(4,128)(2,1)S(1)}, bf16[4,4096]{1,0:T(4,128)(2,1)S(1)}, u32[]{:S(2)}, u32[]{:S(2)}) collective-permute-start(bf16[4,4096]{1,0:T(4,128)(2,1)S(1)} %fusion.19), channel_id=1, source_target_pairs={{0,4},{4,8},{8,12},{12,16},{16,20},{20,24},{24,28},{28,0},{1,5},{5... | collective-permute-start | bytes 98312 | tf_op jit(solution)/shard_map/ppermute | solution.py:40
  16.3 6.6 %collective-permute-start.1 = (bf16[4,4096]{1,0:T(4,128)(2,1)S(1)}, bf16[4,4096]{1,0:T(4,128)(2,1)S(1)}, u32[]{:S(2)}, u32[]{:S(2)}) collective-permute-start(bf16[4,4096]{1,0:T(4,128)(2,1)S(1)} %collective-permute-done), channel_id=1, source_target_pairs={{0,4},{4,8},{8,12},{12,16},{16,20},{20,24},{24,28},{28,0},{1,5},{5... | collective-permute-start | bytes 98312 | tf_op jit(solution)/shard_map/ppermute | solution.py:40
  22.9 8.1 %collective-permute-start.2 = (bf16[4,4096]{1,0:T(4,128)(2,1)S(1)}, bf16[4,4096]{1,0:T(4,128)(2,1)S(1)}, u32[]{:S(2)}, u32[]{:S(2)}) collective-permute-start(bf16[4,4096]{1,0:T(4,128)(2,1)S(1)} %collective-permute-done.1), channel_id=1, source_target_pairs={{0,4},{4,8},{8,12},{12,16},{16,20},{20,24},{24,28},{28,0},{1,5},{5... | collective-permute-start | bytes 98312 | tf_op jit(solution)/shard_map/ppermute | solution.py:40
  25.0 43.2 %all-to-all-start = ((bf16[8,6,4096]{2,1,0:T(8,128)(2,1)}), bf16[8,6,4096]{2,1,0:T(8,128)(2,1)S(1)}, u32[]{:S(2)}, u32[]{:S(2)}) async-start(bf16[8,6,4096]{2,1,0:T(8,128)(2,1)} %reshape_broadcast_in_dim_reshape.3), calls=%async_computation | async-start | bytes 1048576 | tf_op jit(solution)/shard_map/all_to_all | solution.py:70
  31.0 12.0 %collective-permute-start.3 = (bf16[4,4096]{1,0:T(4,128)(2,1)S(1)}, bf16[4,4096]{1,0:T(4,128)(2,1)S(1)}, u32[]{:S(2)}, u32[]{:S(2)}) collective-permute-start(bf16[4,4096]{1,0:T(4,128)(2,1)S(1)} %collective-permute-done.2), channel_id=1, source_target_pairs={{0,4},{4,8},{8,12},{12,16},{16,20},{20,24},{24,28},{28,0},{1,5},{5... | collective-permute-start | bytes 98312 | tf_op jit(solution)/shard_map/ppermute | solution.py:40
  43.1 6.6 %collective-permute-start.4 = (bf16[4,4096]{1,0:T(4,128)(2,1)S(1)}, bf16[4,4096]{1,0:T(4,128)(2,1)S(1)}, u32[]{:S(2)}, u32[]{:S(2)}) collective-permute-start(bf16[4,4096]{1,0:T(4,128)(2,1)S(1)} %collective-permute-done.3), channel_id=1, source_target_pairs={{0,4},{4,8},{8,12},{12,16},{16,20},{20,24},{24,28},{28,0},{1,5},{5... | collective-permute-start | bytes 98312 | tf_op jit(solution)/shard_map/ppermute | solution.py:40
  49.7 6.6 %collective-permute-start.5 = (bf16[4,4096]{1,0:T(4,128)(2,1)S(1)}, bf16[4,4096]{1,0:T(4,128)(2,1)S(1)}, u32[]{:S(2)}, u32[]{:S(2)}) collective-permute-start(bf16[4,4096]{1,0:T(4,128)(2,1)S(1)} %collective-permute-done.4), channel_id=1, source_target_pairs={{0,4},{4,8},{8,12},{12,16},{16,20},{20,24},{24,28},{28,0},{1,5},{5... | collective-permute-start | bytes 98312 | tf_op jit(solution)/shard_map/ppermute | solution.py:40
  56.3 6.6 %collective-permute-start.6 = (bf16[4,4096]{1,0:T(4,128)(2,1)S(1)}, bf16[4,4096]{1,0:T(4,128)(2,1)S(1)}, u32[]{:S(2)}, u32[]{:S(2)}) collective-permute-start(bf16[4,4096]{1,0:T(4,128)(2,1)S(1)} %collective-permute-done.5), channel_id=1, source_target_pairs={{0,4},{4,8},{8,12},{12,16},{16,20},{20,24},{24,28},{28,0},{1,5},{5... | collective-permute-start | bytes 98312 | tf_op jit(solution)/shard_map/ppermute | solution.py:40
  90.8 15.9 %copy-start.2 = (u32[32]{0:T(128)S(1)}, u32[32]{0:T(128)}, u32[]{:S(2)}) copy-start(u32[32]{0:T(128)} %constant.62) | copy-start | bytes 388
  90.9 16.4 %copy-start.1 = (u32[32]{0:T(128)S(1)}, u32[32]{0:T(128)}, u32[]{:S(2)}) copy-start(u32[32]{0:T(128)} %constant.58) | copy-start | bytes 388
  90.9 122.1 %copy-start = (bf16[4,4096]{1,0:T(4,128)(2,1)S(1)}, bf16[4,4096]{1,0:T(4,128)(2,1)}, u32[]{:S(2)}) copy-start(bf16[4,4096]{1,0:T(4,128)(2,1)} %param.12) | copy-start | bytes 98308
  91.8 13.7 %all-to-all-start.1 = ((bf16[8,6,4096]{2,1,0:T(8,128)(2,1)}), bf16[8,6,4096]{2,1,0:T(8,128)(2,1)S(1)}, u32[]{:S(2)}, u32[]{:S(2)}) async-start(bf16[8,6,4096]{2,1,0:T(8,128)(2,1)} %reshape.52), calls=%async_computation.1 | async-start | bytes 1048576 | tf_op jit(solution)/shard_map/all_to_all | solution.py:77
  95.3 83.8 %all-reduce.5.cloned.1.call-start = ((), (), s32[]{:S(2)}) async-start(), calls=%async_computation.2 | async-start | bytes 1048576
  105.0 108.0 %all-reduce.7.cloned.1.call-start = ((), (), s32[]{:S(2)}) async-start(), calls=%async_computation.3 | async-start | bytes 524288
Sparse Core Ops, SparseCore 0:
  105.1 73.9 all-reduce.4
  181.5 31.4 all-reduce.6
